TPU v7x, 32 devices: a whole 2x2x4 slice. The times are simulated.
32 devices in a mesh: ep: 4 (over x, core), tp: 8 (over z, y).
Axes of the slice: x: 2, y: 2, z: 4, core: 2. Of those that a mesh axis runs over, the one named last changes fastest.
Arguments:
- tokens: bfloat16 [32, 3072], P(('ep', 'tp')), may hold values from -6 to 6
- cotangent: bfloat16 [32, 3072], P(('ep', 'tp')), may hold values from -6 to 6
- routes: int32 [32, 2], P(('ep', 'tp')), may hold values from 0 to 3, as said below
- gate_weights: bfloat16 [32, 2], P(('ep', 'tp')), may hold values from 0.099609375 to 1
- w_gate: bfloat16 [4, 3072, 8192], P('ep', None, 'tp'), may hold values from -0.109375 to 0.109375
- w_up: bfloat16 [4, 3072, 8192], P('ep', None, 'tp'), may hold values from -0.109375 to 0.109375
- w_down: bfloat16 [4, 8192, 3072], P('ep', 'tp'), may hold values from -0.0625 to 0.0625
Outputs:
- layer_out: bfloat16 [32, 3072], P(('ep', 'tp'))
- grad_tokens: bfloat16 [32, 3072], P(('ep', 'tp'))
- grad_gate: bfloat16 [4, 3072, 8192], P('ep', None, 'tp')
- grad_up: bfloat16 [4, 3072, 8192], P('ep', None, 'tp')
- grad_down: bfloat16 [4, 8192, 3072], P('ep', 'tp')
Inputs may be any that keep to these rules, and one draw needn't show every extreme that they name: `routes`: each token names two different experts. One expert is named by exactly 28 tokens; every other expert by at most 14 tokens, and one of them by exactly 14.
All inputs are finite; a program needn't handle non-finite values.
Results may differ from a plain program's by a relative error of at most 0.005.
Values may be sent and summed in bfloat16 or wider, within the bound.
A program may use at most 128 MiB of HBM per device.

v0:
```python
import functools

import jax
import jax.numpy as jnp
from jax import lax
from jax.experimental import pallas as pl
from jax.experimental.pallas import tpu as pltpu
from jax.sharding import PartitionSpec as P

LANES = 128
PIECE = 16
MESH = pl.DeviceIdType.MESH


def up_to(value, step):
    return -(-value // step) * step


def dot_nn(left, right):
    return lax.dot_general(left, right, (((1,), (0,)), ((), ())), preferred_element_type=jnp.float32)


def dot_nt(left, right):
    return lax.dot_general(left, right, (((1,), (1,)), ((), ())), preferred_element_type=jnp.float32)


def dot_tn(left, right):
    return lax.dot_general(left, right, (((0,), (0,)), ((), ())), preferred_element_type=jnp.float32)


def expert_kernel(
    n_ep, n_tp, own, pad,
    tokens_ref, cotan_ref, routes_ref, gates_ref, wg_hbm, wu_hbm, wd_hbm,
    tok, cot, hid, ggp, gup, res,
    row32, gath, flat, wg, wu, wd, snd32, snd, pair, half, rcv,
    w_sem, ag_send, ag_recv, fw_send, fw_recv, pr_send, pr_recv, rs_send, rs_recv,
):
    ep, tp = lax.axis_index("ep"), lax.axis_index("tp")
    side, col = lax.rem(ep, 2), ep // 2
    n_half = n_ep * n_tp // 2
    mine = col * n_tp + tp
    partner = (2 * col + 1 - side, tp)
    total, model = tok.shape
    groups = model // LANES
    n_chunks, _, width = wg.shape
    n_pieces = snd.shape[0]

    def peer(step):
        other = lax.rem(mine + step, n_half)
        return (2 * (other // n_tp) + side, lax.rem(other, n_tp))

    barrier = pltpu.get_barrier_semaphore()
    pl.semaphore_signal(barrier, inc=1, device_id=partner, device_id_type=MESH)

    @pl.loop(1, n_half)
    def _(step):
        pl.semaphore_signal(barrier, inc=1, device_id=peer(step), device_id_type=MESH)

    def weight_copies(c):
        columns = pl.ds(pl.multiple_of(c * width, width), width)
        return (
            pltpu.make_async_copy(wg_hbm.at[:, columns], wg.at[c], w_sem.at[0, c]),
            pltpu.make_async_copy(wu_hbm.at[:, columns], wu.at[c], w_sem.at[1, c]),
            pltpu.make_async_copy(wd_hbm.at[columns, :], wd.at[c], w_sem.at[2, c]),
        )

    for c in range(n_chunks):
        for copy in weight_copies(c):
            copy.start()

    row32[...] = jnp.zeros_like(row32)
    ids = lax.broadcasted_iota(jnp.int32, (1, LANES), 1)
    for r in range(own):
        for j in range(groups):
            lanes = slice(j * LANES, (j + 1) * LANES)
            at = r * pad + j
            row32[at:at + 1, :] = tokens_ref[r:r + 1, lanes].astype(jnp.float32)
            row32[at + groups:at + groups + 1, :] = cotan_ref[r:r + 1, lanes].astype(jnp.float32)
        gates = jnp.zeros((1, LANES), jnp.float32)
        for k in range(routes_ref.shape[1]):
            chosen = ids == routes_ref[r:r + 1, k:k + 1]
            gates = gates + jnp.where(chosen, gates_ref[r:r + 1, k:k + 1].astype(jnp.float32), 0.0)
        at = r * pad + 2 * groups
        row32[at:at + 1, :] = gates
    gath[0, 0] = row32[...].astype(jnp.bfloat16)

    pl.semaphore_wait(barrier, n_half)

    @pl.loop(1, n_half)
    def _(step):
        pltpu.make_async_remote_copy(
            src_ref=gath.at[0, 0], dst_ref=gath.at[0, step], send_sem=ag_send, recv_sem=ag_recv,
            device_id=peer(step), device_id_type=MESH,
        ).start()

    block = own * pad
    others = pl.ds(1, n_half - 1)
    pltpu.make_async_copy(gath.at[0, others], gath.at[0, others], ag_recv).wait()
    forward = pltpu.make_async_remote_copy(
        src_ref=gath.at[0], dst_ref=gath.at[1], send_sem=fw_send, recv_sem=fw_recv,
        device_id=partner, device_id_type=MESH,
    )
    forward.start()

    def spread(which, its_side):
        @pl.loop(0, n_half)
        def _(step):
            source = lax.rem(mine + n_half - step, n_half)
            device = (2 * (source // n_tp) + its_side) * n_tp + lax.rem(source, n_tp)
            flat[pl.ds(pl.multiple_of(device * block, 8), block), :] = (
                gath[which, step].astype(jnp.float32)
            )

    spread(0, side)
    forward.wait_recv()
    spread(1, 1 - side)

    for j in range(groups):
        tok[:, j * LANES:(j + 1) * LANES] = flat[pl.ds(j, total, stride=pad), :].astype(jnp.bfloat16)
        cot[:, j * LANES:(j + 1) * LANES] = flat[pl.ds(groups + j, total, stride=pad), :].astype(jnp.bfloat16)
    gate_rows = flat[pl.ds(2 * groups, total, stride=pad), :]
    lane = lax.broadcasted_iota(jnp.int32, gate_rows.shape, 1)
    gate = jnp.sum(jnp.where(lane == ep, gate_rows, 0.0), axis=1, keepdims=True)

    @pl.loop(0, n_chunks)
    def _(c):
        for copy in weight_copies(c):
            copy.wait()
        gate_pre = dot_nn(tok[...], wg[c])
        up_pre = dot_nn(tok[...], wu[c])
        grad_act = dot_nt(cot[...], wd[c]) * gate
        sigmoid = jax.nn.sigmoid(gate_pre)
        silu = gate_pre * sigmoid
        columns = pl.ds(pl.multiple_of(c * width, width), width)
        hid[:, columns] = (silu * up_pre * gate).astype(jnp.bfloat16)
        ggp[:, columns] = (
            grad_act * up_pre * (sigmoid * (1.0 + gate_pre * (1.0 - sigmoid)))
        ).astype(jnp.bfloat16)
        gup[:, columns] = (grad_act * silu).astype(jnp.bfloat16)

    def pair_copy(p):
        return pltpu.make_async_remote_copy(
            src_ref=snd.at[p, 1 - side], dst_ref=pair.at[p],
            send_sem=pr_send.at[p], recv_sem=pr_recv.at[p],
            device_id=partner, device_id_type=MESH,
        )

    def home_copies(p):
        pair_copy(p).wait_recv()
        half[p] = (
            snd[p, side].astype(jnp.float32) + pair[p].astype(jnp.float32)
        ).astype(jnp.bfloat16)

        @pl.loop(1, n_half)
        def _(step):
            pltpu.make_async_remote_copy(
                src_ref=half.at[p, lax.rem(mine + step, n_half)], dst_ref=rcv.at[p, step - 1],
                send_sem=rs_send.at[p], recv_sem=rs_recv.at[p],
                device_id=peer(step), device_id_type=MESH,
            ).start()

    unit = min(4, groups)
    for p in range(n_pieces):
        for first in range(p * PIECE, min((p + 1) * PIECE, 2 * groups), unit):
            start = (first % groups) * LANES
            cols = slice(start, start + unit * LANES)
            value = None
            for c in range(n_chunks):
                inner = slice(c * width, (c + 1) * width)
                if first < groups:
                    term = dot_nn(hid[:, inner], wd[c, :, cols])
                else:
                    term = dot_nt(ggp[:, inner], wg[c, cols, :]) + dot_nt(gup[:, inner], wu[c, cols, :])
                value = term if value is None else value + term
            for k in range(unit):
                snd32[pl.ds(first - p * PIECE + k, total, stride=PIECE), :] = (
                    value[:, k * LANES:(k + 1) * LANES]
                )
        for d in range(2 * n_half):
            d_ep, d_tp = divmod(d, n_tp)
            snd[p, d_ep % 2, (d_ep // 2) * n_tp + d_tp] = (
                snd32[d * own * PIECE:(d + 1) * own * PIECE, :].astype(jnp.bfloat16)
            )
        pair_copy(p).start()
        if p > 0:
            home_copies(p - 1)
    home_copies(n_pieces - 1)

    for p in range(n_pieces):
        pltpu.make_async_copy(rcv.at[p], rcv.at[p], rs_recv.at[p]).wait()
        res[p] = lax.fori_loop(
            0, n_half - 1, lambda s, acc: acc + rcv[p, s].astype(jnp.float32),
            half[p, mine].astype(jnp.float32),
        )
    pltpu.make_async_copy(gath.at[0, others], gath.at[0, others], ag_send).wait()
    forward.wait_send()
    for p in range(n_pieces):
        pair_copy(p).wait_send()
        pltpu.make_async_copy(rcv.at[p], rcv.at[p], rs_send.at[p]).wait()


def weight_kernel(own, tok, cot, hid, ggp, gup, res, dg, du, dd, out, dtok):
    dg[...] = dot_tn(tok[...], ggp[...]).astype(jnp.bfloat16)
    du[...] = dot_tn(tok[...], gup[...]).astype(jnp.bfloat16)
    dd[...] = dot_tn(hid[...], cot[...]).astype(jnp.bfloat16)

    @pl.when(pl.program_id(0) == 0)
    def _():
        groups = out.shape[1] // LANES
        for r in range(own):
            for j in range(2 * groups):
                line = res[j // PIECE, r * PIECE + j % PIECE:r * PIECE + j % PIECE + 1, :]
                k = j % groups
                ref = out if j < groups else dtok
                ref[r:r + 1, k * LANES:(k + 1) * LANES] = line.astype(jnp.bfloat16)


def on_device(n_ep, n_tp, tokens, cotangent, routes, gate_weights, w_gate, w_up, w_down):
    n = n_ep * n_tp
    own, model = tokens.shape
    hidden = w_gate.shape[2]
    total = own * n
    groups = model // LANES
    used = 2 * groups + 1
    pad = up_to(used, PIECE)
    width = min(256, hidden)
    n_chunks = hidden // width
    n_pieces = up_to(2 * groups, PIECE) // PIECE

    vmem = pl.BlockSpec(memory_space=pltpu.VMEM)
    hbm = pl.BlockSpec(memory_space=pl.ANY)
    bf16 = jnp.bfloat16
    n_half = n // 2
    tok, cot, hid, ggp, gup, res = pl.pallas_call(
        functools.partial(expert_kernel, n_ep, n_tp, own, pad),
        out_shape=(
            jax.ShapeDtypeStruct((total, model), bf16),
            jax.ShapeDtypeStruct((total, model), bf16),
            jax.ShapeDtypeStruct((total, hidden), bf16),
            jax.ShapeDtypeStruct((total, hidden), bf16),
            jax.ShapeDtypeStruct((total, hidden), bf16),
            jax.ShapeDtypeStruct((n_pieces, own * PIECE, LANES), jnp.float32),
        ),
        in_specs=[vmem] * 4 + [hbm] * 3,
        out_specs=(vmem,) * 6,
        scratch_shapes=[
            pltpu.VMEM((own * pad, LANES), jnp.float32),
            pltpu.VMEM((2, n_half, own * pad, LANES), bf16),
            pltpu.VMEM((total * pad, LANES), jnp.float32),
            pltpu.VMEM((n_chunks, model, width), bf16),
            pltpu.VMEM((n_chunks, model, width), bf16),
            pltpu.VMEM((n_chunks, width, model), bf16),
            pltpu.VMEM((total * PIECE, LANES), jnp.float32),
            pltpu.VMEM((n_pieces, 2, n_half, own * PIECE, LANES), bf16),
            pltpu.VMEM((n_pieces, n_half, own * PIECE, LANES), bf16),
            pltpu.VMEM((n_pieces, n_half, own * PIECE, LANES), bf16),
            pltpu.VMEM((n_pieces, n_half - 1, own * PIECE, LANES), bf16),
            pltpu.SemaphoreType.DMA((3, n_chunks)),
            pltpu.SemaphoreType.DMA,
            pltpu.SemaphoreType.DMA,
            pltpu.SemaphoreType.DMA,
            pltpu.SemaphoreType.DMA,
            pltpu.SemaphoreType.DMA((n_pieces,)),
            pltpu.SemaphoreType.DMA((n_pieces,)),
            pltpu.SemaphoreType.DMA((n_pieces,)),
            pltpu.SemaphoreType.DMA((n_pieces,)),
        ],
        compiler_params=pltpu.CompilerParams(
            collective_id=0, has_side_effects=True, vmem_limit_bytes=56 * 2**20
        ),
        name="expert",
    )(tokens, cotangent, routes, gate_weights, w_gate[0], w_up[0], w_down[0])

    step = 384 if model % 384 == 0 else LANES
    whole = pl.BlockSpec((total, hidden), lambda i: (0, 0))
    rows = pl.BlockSpec((total, step), lambda i: (0, i))
    flat_out = pl.BlockSpec((own, model), lambda i: (0, 0))
    dg, du, dd, out, dtok = pl.pallas_call(
        functools.partial(weight_kernel, own),
        grid=(model // step,),
        out_shape=(
            jax.ShapeDtypeStruct((model, hidden), bf16),
            jax.ShapeDtypeStruct((model, hidden), bf16),
            jax.ShapeDtypeStruct((hidden, model), bf16),
            jax.ShapeDtypeStruct((own, model), bf16),
            jax.ShapeDtypeStruct((own, model), bf16),
        ),
        in_specs=[
            rows, rows, whole, whole, whole,
            pl.BlockSpec((n_pieces, own * PIECE, LANES), lambda i: (0, 0, 0)),
        ],
        out_specs=(
            pl.BlockSpec((step, hidden), lambda i: (i, 0)),
            pl.BlockSpec((step, hidden), lambda i: (i, 0)),
            pl.BlockSpec((hidden, step), lambda i: (0, i)),
            flat_out,
            flat_out,
        ),
        compiler_params=pltpu.CompilerParams(vmem_limit_bytes=60 * 2**20),
        name="weights",
    )(tok, cot, hid, ggp, gup, res)

    return (out, dtok, dg[None], du[None], dd[None])


def solution(mesh):
    placed = (
        P(("ep", "tp"), None),
        P(("ep", "tp"), None),
        P(("ep", "tp"), None),
        P(("ep", "tp"), None),
        P("ep", None, "tp"),
        P("ep", None, "tp"),
        P("ep", "tp", None),
    )
    return jax.shard_map(
        functools.partial(on_device, mesh.shape["ep"], mesh.shape["tp"]),
        mesh=mesh,
        in_specs=placed,
        out_specs=(
            P(("ep", "tp"), None),
            P(("ep", "tp"), None),
            P("ep", None, "tp"),
            P("ep", None, "tp"),
            P("ep", "tp", None),
        ),
        check_vma=False,
    )
```

profile of v0, /device:TPU:0, one launch (start us, length us, event | category | flops | bytes accessed | tf_op | source)
XLA Modules:
  0.0 45.2 jit_solution(2148652271637091093)
XLA Ops:
  0.6 34.0 %expert.1 = (bf16[32,3072]{1,0:T(8,128)(2,1)}, bf16[32,3072]{1,0:T(8,128)(2,1)}, bf16[32,1024]{1,0:T(8,128)(2,1)}, bf16[32,1024]{1,0:T(8,128)(2,1)}, bf16[32,1024]{1,0:T(8,128)(2,1)}, /*index=5*/f32[3,16,128]{2,1,0:T(8,128)}) custom-call(bf16[1,3072]{1,0:T(2,128)(2,1)} %tokens_ref.1, bf16[1,3072]{1,0:T(2,128)(2,1)} %cotan_ref.1, s32[1,2]{1,0:T(1,128)} %routes_ref.1, ...), custom_call_target="tpu_custom_call" | custom-call | tf_op jit(solution)/shard_map/expert/pallas_call | solution.py:234
  34.7 10.5 %weights.1 = (bf16[3072,1024]{1,0:T(8,128)(2,1)}, bf16[3072,1024]{1,0:T(8,128)(2,1)}, bf16[1024,3072]{1,0:T(8,128)(2,1)}, bf16[1,3072]{1,0:T(2,128)(2,1)}, bf16[1,3072]{1,0:T(2,128)(2,1)}) custom-call(bf16[32,3072]{1,0:T(8,128)(2,1)} %get-tuple-element.16.tok, bf16[32,3072]{1,0:T(8,128)(2,1)} %get-tuple-element.17.cot, ...), custom_call_target="tpu_custom_call" | custom-call | tf_op jit(solution)/shard_map/weights/pallas_call | solution.py:278
where the time goes:
time: 45.6 us; the launch traced here: 45.2 us
  Pallas kernels  44.5 us (98%)
  between operations  0.64 us (1%)
    pallas_call x1, Pallas kernels, on_device(): pl.pallas_call(functools.partial(expert_kernel, n_ep, n_tp, own, pad), ou...  34 us
    pallas_call x1, Pallas kernels, on_device(): pl.pallas_call(functools.partial(weight_kernel, own), grid=(model // step...  10.5 us

commit v1 on v0

--- a/solution.py
+++ b/solution.py
@@ -199,20 +199,35 @@
         pltpu.make_async_copy(rcv.at[p], rcv.at[p], rs_send.at[p]).wait()
 
 
-def weight_kernel(own, tok, cot, hid, ggp, gup, res, dg, du, dd, out, dtok):
-    dg[...] = dot_tn(tok[...], ggp[...]).astype(jnp.bfloat16)
-    du[...] = dot_tn(tok[...], gup[...]).astype(jnp.bfloat16)
-    dd[...] = dot_tn(hid[...], cot[...]).astype(jnp.bfloat16)
-
-    @pl.when(pl.program_id(0) == 0)
-    def _():
-        groups = out.shape[1] // LANES
-        for r in range(own):
-            for j in range(2 * groups):
-                line = res[j // PIECE, r * PIECE + j % PIECE:r * PIECE + j % PIECE + 1, :]
-                k = j % groups
-                ref = out if j < groups else dtok
-                ref[r:r + 1, k * LANES:(k + 1) * LANES] = line.astype(jnp.bfloat16)
+def weight_kernel(own, tok, cot, hid, ggp, gup, res, dg_hbm, du_hbm, dd_hbm, out, dtok, dg, du, dd, sem):
+    model, hidden = dg.shape
+    tall = 192 if model % 192 == 0 else LANES
+    wide = min(LANES, hidden)
+    n_tall, n_wide = model // tall, hidden // wide
+    done = 0
+    for i in range(n_tall):
+        rows = slice(i * tall, (i + 1) * tall)
+        dg[rows, :] = dot_tn(tok[:, rows], ggp[...]).astype(jnp.bfloat16)
+        pltpu.make_async_copy(dg.at[rows], dg_hbm.at[rows], sem.at[0]).start()
+        du[rows, :] = dot_tn(tok[:, rows], gup[...]).astype(jnp.bfloat16)
+        pltpu.make_async_copy(du.at[rows], du_hbm.at[rows], sem.at[1]).start()
+        while done * n_tall < (i + 1) * n_wide:
+            lines = slice(done * wide, (done + 1) * wide)
+            dd[lines, :] = dot_tn(hid[:, lines], cot[...]).astype(jnp.bfloat16)
+            pltpu.make_async_copy(dd.at[lines], dd_hbm.at[lines], sem.at[2]).start()
+            done += 1
+
+    groups = out.shape[1] // LANES
+    for r in range(own):
+        for j in range(2 * groups):
+            line = res[j // PIECE, r * PIECE + j % PIECE:r * PIECE + j % PIECE + 1, :]
+            k = j % groups
+            ref = out if j < groups else dtok
+            ref[r:r + 1, k * LANES:(k + 1) * LANES] = line.astype(jnp.bfloat16)
+
+    pltpu.make_async_copy(dg, dg_hbm, sem.at[0]).wait()
+    pltpu.make_async_copy(du, du_hbm, sem.at[1]).wait()
+    pltpu.make_async_copy(dd, dd_hbm, sem.at[2]).wait()
 
 
 def on_device(n_ep, n_tp, tokens, cotangent, routes, gate_weights, w_gate, w_up, w_down):
@@ -271,13 +286,8 @@
         name="expert",
     )(tokens, cotangent, routes, gate_weights, w_gate[0], w_up[0], w_down[0])
 
-    step = 384 if model % 384 == 0 else LANES
-    whole = pl.BlockSpec((total, hidden), lambda i: (0, 0))
-    rows = pl.BlockSpec((total, step), lambda i: (0, i))
-    flat_out = pl.BlockSpec((own, model), lambda i: (0, 0))
     dg, du, dd, out, dtok = pl.pallas_call(
         functools.partial(weight_kernel, own),
-        grid=(model // step,),
         out_shape=(
             jax.ShapeDtypeStruct((model, hidden), bf16),
             jax.ShapeDtypeStruct((model, hidden), bf16),
@@ -285,17 +295,14 @@
             jax.ShapeDtypeStruct((own, model), bf16),
             jax.ShapeDtypeStruct((own, model), bf16),
         ),
-        in_specs=[
-            rows, rows, whole, whole, whole,
-            pl.BlockSpec((n_pieces, own * PIECE, LANES), lambda i: (0, 0, 0)),
+        in_specs=[vmem] * 6,
+        out_specs=(hbm,) * 3 + (vmem,) * 2,
+        scratch_shapes=[
+            pltpu.VMEM((model, hidden), bf16),
+            pltpu.VMEM((model, hidden), bf16),
+            pltpu.VMEM((hidden, model), bf16),
+            pltpu.SemaphoreType.DMA((3,)),
         ],
-        out_specs=(
-            pl.BlockSpec((step, hidden), lambda i: (i, 0)),
-            pl.BlockSpec((step, hidden), lambda i: (i, 0)),
-            pl.BlockSpec((hidden, step), lambda i: (0, i)),
-            flat_out,
-            flat_out,
-        ),
         compiler_params=pltpu.CompilerParams(vmem_limit_bytes=60 * 2**20),
         name="weights",
     )(tok, cot, hid, ggp, gup, res)

time: 45.6 us -> 43.4 us (0.952)
  Pallas kernels: 44.5 us -> 42.5 us
    pallas_call x1, Pallas kernels: 10.5 us -> 8.5 us  [on_device(): pl.pallas_call(functools.partial(weight_kernel, own), out_shape=(jax.Shap...]
where the time goes in v1:
time: 43.4 us; the launch traced here: 43.2 us
  Pallas kernels  42.5 us (98%)
  between operations  0.64 us (1%)
    pallas_call x1, Pallas kernels, on_device(): pl.pallas_call(functools.partial(expert_kernel, n_ep, n_tp, own, pad), ou...  34 us
    pallas_call x1, Pallas kernels, on_device(): pl.pallas_call(functools.partial(weight_kernel, own), out_shape=(jax.Shap...  8.5 us

profile of v1, /device:TPU:0, one launch (start us, length us, event | category | flops | bytes accessed | tf_op | source)
XLA Modules:
  0.0 43.2 jit_solution(8337844930096790701)
XLA Ops:
  0.6 34.0 %expert.1 = (bf16[32,3072]{1,0:T(8,128)(2,1)}, bf16[32,3072]{1,0:T(8,128)(2,1)}, bf16[32,1024]{1,0:T(8,128)(2,1)}, bf16[32,1024]{1,0:T(8,128)(2,1)}, bf16[32,1024]{1,0:T(8,128)(2,1)}, /*index=5*/f32[3,16,128]{2,1,0:T(8,128)}) custom-call(bf16[1,3072]{1,0:T(2,128)(2,1)} %tokens_ref.1, bf16[1,3072]{1,0:T(2,128)(2,1)} %cotan_ref.1, s32[1,2]{1,0:T(1,128)} %routes_ref.1, ...), custom_call_target="tpu_custom_call" | custom-call | tf_op jit(solution)/shard_map/expert/pallas_call | solution.py:249
  34.7 8.5 %weights.1 = (bf16[3072,1024]{1,0:T(8,128)(2,1)}, bf16[3072,1024]{1,0:T(8,128)(2,1)}, bf16[1024,3072]{1,0:T(8,128)(2,1)}, bf16[1,3072]{1,0:T(2,128)(2,1)}, bf16[1,3072]{1,0:T(2,128)(2,1)}) custom-call(bf16[32,3072]{1,0:T(8,128)(2,1)} %get-tuple-element.16.tok, bf16[32,3072]{1,0:T(8,128)(2,1)} %get-tuple-element.17.cot, ...), custom_call_target="tpu_custom_call" | custom-call | tf_op jit(solution)/shard_map/weights/pallas_call | solution.py:289

commit v2 on v1

--- a/solution.py
+++ b/solution.py
@@ -86,12 +86,26 @@
 
     pl.semaphore_wait(barrier, n_half)
 
-    @pl.loop(1, n_half)
-    def _(step):
-        pltpu.make_async_remote_copy(
-            src_ref=gath.at[0, 0], dst_ref=gath.at[0, step], send_sem=ag_send, recv_sem=ag_recv,
-            device_id=peer(step), device_id_type=MESH,
-        ).start()
+    n_layers = 1
+    while n_layers * n_layers < n_tp:
+        n_layers *= 2
+    per = n_tp // n_layers
+    spots = n_half // n_layers
+    low = tp // per < n_layers // 2
+
+    @pl.loop(0, n_half)
+    def _(turn):
+        its_layer = jnp.where(low, n_layers - 1 - turn // spots, turn // spots)
+        its_spot = lax.rem(mine + turn, spots)
+        other = (its_spot // per) * n_tp + its_layer * per + lax.rem(its_spot, per)
+        step = lax.rem(other - mine + n_half, n_half)
+
+        @pl.when(step != 0)
+        def _():
+            pltpu.make_async_remote_copy(
+                src_ref=gath.at[0, 0], dst_ref=gath.at[0, step], send_sem=ag_send, recv_sem=ag_recv,
+                device_id=peer(step), device_id_type=MESH,
+            ).start()
 
     block = own * pad
     others = pl.ds(1, n_half - 1)
@@ -237,7 +251,7 @@
     total = own * n
     groups = model // LANES
     used = 2 * groups + 1
-    pad = up_to(used, PIECE)
+    pad = up_to(used, 8)
     width = min(256, hidden)
     n_chunks = hidden // width
     n_pieces = up_to(2 * groups, PIECE) // PIECE
@@ -249,12 +263,12 @@
     tok, cot, hid, ggp, gup, res = pl.pallas_call(
         functools.partial(expert_kernel, n_ep, n_tp, own, pad),
         out_shape=(
-            jax.ShapeDtypeStruct((total, model), bf16),
-            jax.ShapeDtypeStruct((total, model), bf16),
-            jax.ShapeDtypeStruct((total, hidden), bf16),
-            jax.ShapeDtypeStruct((total, hidden), bf16),
-            jax.ShapeDtypeStruct((total, hidden), bf16),
-            jax.ShapeDtypeStruct((n_pieces, own * PIECE, LANES), jnp.float32),
+            pltpu.VMEM((total, model), bf16),
+            pltpu.VMEM((total, model), bf16),
+            pltpu.VMEM((total, hidden), bf16),
+            pltpu.VMEM((total, hidden), bf16),
+            pltpu.VMEM((total, hidden), bf16),
+            pltpu.VMEM((n_pieces, own * PIECE, LANES), jnp.float32),
         ),
         in_specs=[vmem] * 4 + [hbm] * 3,
         out_specs=(vmem,) * 6,
@@ -305,7 +319,7 @@
         ],
         compiler_params=pltpu.CompilerParams(vmem_limit_bytes=60 * 2**20),
         name="weights",
-    )(tok, cot, hid, ggp, gup, res)
+    )(*(pltpu.with_memory_space_constraint(x, pltpu.VMEM) for x in (tok, cot, hid, ggp, gup, res)))
 
     return (out, dtok, dg[None], du[None], dd[None])
 

time: 43.4 us -> 39.7 us (0.915)
  Pallas kernels: 42.5 us -> 38.8 us
    pallas_call x1, Pallas kernels: 34 us -> 31.4 us  [on_device(): pl.pallas_call(functools.partial(expert_kernel, n_ep, n_tp, own, pad), ou...]
    pallas_call x1, Pallas kernels: 8.5 us -> 7.38 us  [on_device(): pl.pallas_call(functools.partial(weight_kernel, own), out_shape=(jax.Shap...]
where the time goes in v2:
time: 39.7 us; the launch traced here: 39.4 us
  Pallas kernels  38.8 us (98%)
  between operations  0.64 us (2%)
    pallas_call x1, Pallas kernels, on_device(): pl.pallas_call(functools.partial(expert_kernel, n_ep, n_tp, own, pad), ou...  31.4 us
    pallas_call x1, Pallas kernels, on_device(): pl.pallas_call(functools.partial(weight_kernel, own), out_shape=(jax.Shap...  7.38 us

profile of v2, /device:TPU:0, one launch (start us, length us, event | category | flops | bytes accessed | tf_op | source)
XLA Modules:
  0.0 39.4 jit_solution(828306659611872747)
XLA Ops:
  0.6 31.4 %expert.1 = (bf16[32,3072]{1,0:T(8,128)(2,1)S(1)}, bf16[32,3072]{1,0:T(8,128)(2,1)S(1)}, bf16[32,1024]{1,0:T(8,128)(2,1)S(1)}, bf16[32,1024]{1,0:T(8,128)(2,1)S(...) custom-call(bf16[1,3072]{1,0:T(2,128)(2,1)} %tokens_ref.1, bf16[1,3072]{1,0:T(2,128)(2,1)} %cotan_ref.1, ...), custom_call_target="tpu_custom_call" | custom-call | tf_op jit(solution)/shard_map/expert/pallas_call | solution.py:263
  32.1 7.4 %weights.1 = (bf16[3072,1024]{1,0:T(8,128)(2,1)}, bf16[3072,1024]{1,0:T(8,128)(2,1)}, bf16[1024,3072]{1,0:T(8,128)(2,1)}, bf16[1,3072]{1,0:T(2,128)(2,1)}, bf16[1,3072]{1,0:T(2,128)(2,1)}) custom-call(bf16[32,3072]{1,0:T(8,128)(2,1)S(1)} %get-tuple-element.16.tok, bf16[32,3072]{1,0:T(8,128)(2,1)S(1)} %get-tuple-element.17.cot, ...), custom_call_target="tpu_custom_call" | custom-call | tf_op jit(solution)/shard_map/weights/pallas_call | solution.py:303

commit v3 on v2

--- a/solution.py
+++ b/solution.py
@@ -8,8 +8,16 @@
 from jax.sharding import PartitionSpec as P
 
 LANES = 128
-PIECE = 16
 MESH = pl.DeviceIdType.MESH
+
+
+def cut(total):
+    sizes = []
+    for share in (2, 3):
+        size = max(8, total // share // 8 * 8)
+        if sum(sizes) + size < total:
+            sizes.append(size)
+    return sizes + [total - sum(sizes)]
 
 
 def up_to(value, step):
@@ -29,11 +37,11 @@
 
 
 def expert_kernel(
-    n_ep, n_tp, own, pad,
-    tokens_ref, cotan_ref, routes_ref, gates_ref, wg_hbm, wu_hbm, wd_hbm,
+    n_ep, n_tp, n_layers, own, pad,
+    tokens_hbm, cotan_hbm, routes_hbm, gates_hbm, wg_hbm, wu_hbm, wd_hbm,
     tok, cot, hid, ggp, gup, res,
-    row32, gath, flat, wg, wu, wd, snd32, snd, pair, half, rcv,
-    w_sem, ag_send, ag_recv, fw_send, fw_recv, pr_send, pr_recv, rs_send, rs_recv,
+    tokens_ref, cotan_ref, routes_ref, gates_ref, row32, gath, flat, wg, wu, wd, snd32, pieces,
+    in_sem, w_sem, ag_send, ag_recv, fw_send, fw_recv, pr_send, pr_recv, rs_send, rs_recv,
 ):
     ep, tp = lax.axis_index("ep"), lax.axis_index("tp")
     side, col = lax.rem(ep, 2), ep // 2
@@ -43,11 +51,26 @@
     total, model = tok.shape
     groups = model // LANES
     n_chunks, _, width = wg.shape
-    n_pieces = snd.shape[0]
+    sizes = cut(2 * groups)
+    n_pieces = len(sizes)
+    snd, pair, half, rcv = pieces
+    per = n_tp // n_layers
+    spots = n_half // n_layers
+    layer = tp // per
+    spot = col * per + lax.rem(tp, per)
 
     def peer(step):
         other = lax.rem(mine + step, n_half)
         return (2 * (other // n_tp) + side, lax.rem(other, n_tp))
+
+    inputs = [
+        pltpu.make_async_copy(src, dst, in_sem.at[i])
+        for i, (src, dst) in enumerate((
+            (tokens_hbm, tokens_ref), (cotan_hbm, cotan_ref), (routes_hbm, routes_ref), (gates_hbm, gates_ref),
+        ))
+    ]
+    for copy in inputs:
+        copy.start()
 
     barrier = pltpu.get_barrier_semaphore()
     pl.semaphore_signal(barrier, inc=1, device_id=partner, device_id_type=MESH)
@@ -69,6 +92,8 @@
             copy.start()
 
     row32[...] = jnp.zeros_like(row32)
+    for copy in inputs:
+        copy.wait()
     ids = lax.broadcasted_iota(jnp.int32, (1, LANES), 1)
     for r in range(own):
         for j in range(groups):
@@ -82,52 +107,61 @@
             gates = gates + jnp.where(chosen, gates_ref[r:r + 1, k:k + 1].astype(jnp.float32), 0.0)
         at = r * pad + 2 * groups
         row32[at:at + 1, :] = gates
-    gath[0, 0] = row32[...].astype(jnp.bfloat16)
+    gath[0, layer, spot] = row32[...].astype(jnp.bfloat16)
 
     pl.semaphore_wait(barrier, n_half)
 
-    n_layers = 1
-    while n_layers * n_layers < n_tp:
-        n_layers *= 2
-    per = n_tp // n_layers
-    spots = n_half // n_layers
-    low = tp // per < n_layers // 2
+    low = layer < n_layers // 2
+    own_block = gath.at[0, layer, spot]
 
     @pl.loop(0, n_half)
     def _(turn):
         its_layer = jnp.where(low, n_layers - 1 - turn // spots, turn // spots)
-        its_spot = lax.rem(mine + turn, spots)
-        other = (its_spot // per) * n_tp + its_layer * per + lax.rem(its_spot, per)
-        step = lax.rem(other - mine + n_half, n_half)
-
-        @pl.when(step != 0)
+        its_spot = lax.rem(spot + turn, spots)
+
+        @pl.when((its_layer != layer) | (its_spot != spot))
         def _():
             pltpu.make_async_remote_copy(
-                src_ref=gath.at[0, 0], dst_ref=gath.at[0, step], send_sem=ag_send, recv_sem=ag_recv,
-                device_id=peer(step), device_id_type=MESH,
+                src_ref=own_block, dst_ref=own_block,
+                send_sem=ag_send.at[its_layer], recv_sem=ag_recv.at[layer],
+                device_id=(2 * (its_spot // per) + side, its_layer * per + lax.rem(its_spot, per)),
+                device_id_type=MESH,
             ).start()
 
+    def await_layer(its_layer, sem):
+        @pl.when(its_layer == layer)
+        def _():
+            rest = gath.at[0, its_layer, pl.ds(1, spots - 1)]
+            pltpu.make_async_copy(rest, rest, sem.at[its_layer]).wait()
+
+        @pl.when(its_layer != layer)
+        def _():
+            whole = gath.at[0, its_layer]
+            pltpu.make_async_copy(whole, whole, sem.at[its_layer]).wait()
+
+    def forward(its_layer):
+        return pltpu.make_async_remote_copy(
+            src_ref=gath.at[0, its_layer], dst_ref=gath.at[1, its_layer],
+            send_sem=fw_send.at[its_layer], recv_sem=fw_recv.at[its_layer],
+            device_id=partner, device_id_type=MESH,
+        )
+
     block = own * pad
-    others = pl.ds(1, n_half - 1)
-    pltpu.make_async_copy(gath.at[0, others], gath.at[0, others], ag_recv).wait()
-    forward = pltpu.make_async_remote_copy(
-        src_ref=gath.at[0], dst_ref=gath.at[1], send_sem=fw_send, recv_sem=fw_recv,
-        device_id=partner, device_id_type=MESH,
-    )
-    forward.start()
-
-    def spread(which, its_side):
-        @pl.loop(0, n_half)
-        def _(step):
-            source = lax.rem(mine + n_half - step, n_half)
-            device = (2 * (source // n_tp) + its_side) * n_tp + lax.rem(source, n_tp)
+
+    def spread(which, its_side, its_layer):
+        for its_spot in range(spots):
+            device = (2 * (its_spot // per) + its_side) * n_tp + its_layer * per + its_spot % per
             flat[pl.ds(pl.multiple_of(device * block, 8), block), :] = (
-                gath[which, step].astype(jnp.float32)
+                gath[which, its_layer, its_spot].astype(jnp.float32)
             )
 
-    spread(0, side)
-    forward.wait_recv()
-    spread(1, 1 - side)
+    for its_layer in reversed(range(n_layers)):
+        await_layer(its_layer, ag_recv)
+        forward(its_layer).start()
+        spread(0, side, its_layer)
+    for its_layer in reversed(range(n_layers)):
+        forward(its_layer).wait_recv()
+        spread(1, 1 - side, its_layer)
 
     for j in range(groups):
         tok[:, j * LANES:(j + 1) * LANES] = flat[pl.ds(j, total, stride=pad), :].astype(jnp.bfloat16)
@@ -154,28 +188,28 @@
 
     def pair_copy(p):
         return pltpu.make_async_remote_copy(
-            src_ref=snd.at[p, 1 - side], dst_ref=pair.at[p],
+            src_ref=snd[p].at[1 - side], dst_ref=pair[p],
             send_sem=pr_send.at[p], recv_sem=pr_recv.at[p],
             device_id=partner, device_id_type=MESH,
         )
 
     def home_copies(p):
         pair_copy(p).wait_recv()
-        half[p] = (
-            snd[p, side].astype(jnp.float32) + pair[p].astype(jnp.float32)
+        half[p][...] = (
+            snd[p][side].astype(jnp.float32) + pair[p][...].astype(jnp.float32)
         ).astype(jnp.bfloat16)
 
         @pl.loop(1, n_half)
         def _(step):
             pltpu.make_async_remote_copy(
-                src_ref=half.at[p, lax.rem(mine + step, n_half)], dst_ref=rcv.at[p, step - 1],
+                src_ref=half[p].at[lax.rem(mine + step, n_half)], dst_ref=rcv[p].at[step - 1],
                 send_sem=rs_send.at[p], recv_sem=rs_recv.at[p],
                 device_id=peer(step), device_id_type=MESH,
             ).start()
 
     unit = min(4, groups)
     for p in range(n_pieces):
-        for first in range(p * PIECE, min((p + 1) * PIECE, 2 * groups), unit):
+        for first in range(sum(sizes[:p]), sum(sizes[:p + 1]), unit):
             start = (first % groups) * LANES
             cols = slice(start, start + unit * LANES)
             value = None
@@ -184,16 +218,18 @@
                 if first < groups:
                     term = dot_nn(hid[:, inner], wd[c, :, cols])
                 else:
-                    term = dot_nt(ggp[:, inner], wg[c, cols, :]) + dot_nt(gup[:, inner], wu[c, cols, :])
+                    term = dot_nt(wg[c, cols, :], ggp[:, inner]) + dot_nt(wu[c, cols, :], gup[:, inner])
                 value = term if value is None else value + term
+            if first >= groups:
+                value = value.T
             for k in range(unit):
-                snd32[pl.ds(first - p * PIECE + k, total, stride=PIECE), :] = (
+                snd32[pl.ds(first - sum(sizes[:p]) + k, total, stride=sizes[p]), :] = (
                     value[:, k * LANES:(k + 1) * LANES]
                 )
         for d in range(2 * n_half):
             d_ep, d_tp = divmod(d, n_tp)
-            snd[p, d_ep % 2, (d_ep // 2) * n_tp + d_tp] = (
-                snd32[d * own * PIECE:(d + 1) * own * PIECE, :].astype(jnp.bfloat16)
+            snd[p][d_ep % 2, (d_ep // 2) * n_tp + d_tp] = (
+                snd32[d * own * sizes[p]:(d + 1) * own * sizes[p], :].astype(jnp.bfloat16)
             )
         pair_copy(p).start()
         if p > 0:
@@ -201,16 +237,17 @@
     home_copies(n_pieces - 1)
 
     for p in range(n_pieces):
-        pltpu.make_async_copy(rcv.at[p], rcv.at[p], rs_recv.at[p]).wait()
-        res[p] = lax.fori_loop(
-            0, n_half - 1, lambda s, acc: acc + rcv[p, s].astype(jnp.float32),
-            half[p, mine].astype(jnp.float32),
+        pltpu.make_async_copy(rcv[p], rcv[p], rs_recv.at[p]).wait()
+        res[own * sum(sizes[:p]):own * sum(sizes[:p + 1]), :] = lax.fori_loop(
+            0, n_half - 1, lambda s, acc: acc + rcv[p][s].astype(jnp.float32),
+            half[p][mine].astype(jnp.float32),
         )
-    pltpu.make_async_copy(gath.at[0, others], gath.at[0, others], ag_send).wait()
-    forward.wait_send()
+    for its_layer in range(n_layers):
+        await_layer(its_layer, ag_send)
+        forward(its_layer).wait_send()
     for p in range(n_pieces):
         pair_copy(p).wait_send()
-        pltpu.make_async_copy(rcv.at[p], rcv.at[p], rs_send.at[p]).wait()
+        pltpu.make_async_copy(rcv[p], rcv[p], rs_send.at[p]).wait()
 
 
 def weight_kernel(own, tok, cot, hid, ggp, gup, res, dg_hbm, du_hbm, dd_hbm, out, dtok, dg, du, dd, sem):
@@ -232,12 +269,15 @@
             done += 1
 
     groups = out.shape[1] // LANES
-    for r in range(own):
-        for j in range(2 * groups):
-            line = res[j // PIECE, r * PIECE + j % PIECE:r * PIECE + j % PIECE + 1, :]
-            k = j % groups
-            ref = out if j < groups else dtok
-            ref[r:r + 1, k * LANES:(k + 1) * LANES] = line.astype(jnp.bfloat16)
+    sizes = cut(2 * groups)
+    for p, size in enumerate(sizes):
+        start = sum(sizes[:p])
+        for r in range(own):
+            for j in range(start, start + size):
+                at = own * start + r * size + j - start
+                k = j % groups
+                ref = out if j < groups else dtok
+                ref[r:r + 1, k * LANES:(k + 1) * LANES] = res[at:at + 1, :].astype(jnp.bfloat16)
 
     pltpu.make_async_copy(dg, dg_hbm, sem.at[0]).wait()
     pltpu.make_async_copy(du, du_hbm, sem.at[1]).wait()
@@ -254,41 +294,50 @@
     pad = up_to(used, 8)
     width = min(256, hidden)
     n_chunks = hidden // width
-    n_pieces = up_to(2 * groups, PIECE) // PIECE
+    sizes = cut(2 * groups)
+    n_pieces = len(sizes)
 
     vmem = pl.BlockSpec(memory_space=pltpu.VMEM)
     hbm = pl.BlockSpec(memory_space=pl.ANY)
     bf16 = jnp.bfloat16
     n_half = n // 2
+    n_layers = 1
+    while n_layers * n_layers < n_tp:
+        n_layers *= 2
     tok, cot, hid, ggp, gup, res = pl.pallas_call(
-        functools.partial(expert_kernel, n_ep, n_tp, own, pad),
+        functools.partial(expert_kernel, n_ep, n_tp, n_layers, own, pad),
         out_shape=(
             pltpu.VMEM((total, model), bf16),
             pltpu.VMEM((total, model), bf16),
             pltpu.VMEM((total, hidden), bf16),
             pltpu.VMEM((total, hidden), bf16),
             pltpu.VMEM((total, hidden), bf16),
-            pltpu.VMEM((n_pieces, own * PIECE, LANES), jnp.float32),
+            pltpu.VMEM((own * 2 * groups, LANES), jnp.float32),
         ),
-        in_specs=[vmem] * 4 + [hbm] * 3,
+        in_specs=[hbm] * 7,
         out_specs=(vmem,) * 6,
         scratch_shapes=[
+            pltpu.VMEM(tokens.shape, tokens.dtype),
+            pltpu.VMEM(cotangent.shape, cotangent.dtype),
+            pltpu.VMEM(routes.shape, routes.dtype),
+            pltpu.VMEM(gate_weights.shape, gate_weights.dtype),
             pltpu.VMEM((own * pad, LANES), jnp.float32),
-            pltpu.VMEM((2, n_half, own * pad, LANES), bf16),
+            pltpu.VMEM((2, n_layers, n_half // n_layers, own * pad, LANES), bf16),
             pltpu.VMEM((total * pad, LANES), jnp.float32),
             pltpu.VMEM((n_chunks, model, width), bf16),
             pltpu.VMEM((n_chunks, model, width), bf16),
             pltpu.VMEM((n_chunks, width, model), bf16),
-            pltpu.VMEM((total * PIECE, LANES), jnp.float32),
-            pltpu.VMEM((n_pieces, 2, n_half, own * PIECE, LANES), bf16),
-            pltpu.VMEM((n_pieces, n_half, own * PIECE, LANES), bf16),
-            pltpu.VMEM((n_pieces, n_half, own * PIECE, LANES), bf16),
-            pltpu.VMEM((n_pieces, n_half - 1, own * PIECE, LANES), bf16),
+            pltpu.VMEM((total * max(sizes), LANES), jnp.float32),
+            tuple(
+                [pltpu.VMEM((*lead, own * size, LANES), bf16) for size in sizes]
+                for lead in ((2, n_half), (n_half,), (n_half,), (n_half - 1,))
+            ),
+            pltpu.SemaphoreType.DMA((4,)),
             pltpu.SemaphoreType.DMA((3, n_chunks)),
-            pltpu.SemaphoreType.DMA,
-            pltpu.SemaphoreType.DMA,
-            pltpu.SemaphoreType.DMA,
-            pltpu.SemaphoreType.DMA,
+            pltpu.SemaphoreType.DMA((n_layers,)),
+            pltpu.SemaphoreType.DMA((n_layers,)),
+            pltpu.SemaphoreType.DMA((n_layers,)),
+            pltpu.SemaphoreType.DMA((n_layers,)),
             pltpu.SemaphoreType.DMA((n_pieces,)),
             pltpu.SemaphoreType.DMA((n_pieces,)),
             pltpu.SemaphoreType.DMA((n_pieces,)),

time: 39.7 us -> 38.8 us (0.977)
  Pallas kernels: 38.8 us -> 37.9 us
    pallas_call x1, Pallas kernels: 31.4 us -> 30.5 us  [on_device(): pl.pallas_call(functools.partial(expert_kernel, n_ep, n_tp, n_layers, own...]
where the time goes in v3:
time: 38.8 us; the launch traced here: 38.5 us
  Pallas kernels  37.9 us (98%)
  between operations  0.64 us (2%)
    pallas_call x1, Pallas kernels, on_device(): pl.pallas_call(functools.partial(expert_kernel, n_ep, n_tp, n_layers, own...  30.5 us
    pallas_call x1, Pallas kernels, on_device(): pl.pallas_call(functools.partial(weight_kernel, own), out_shape=(jax.Shap...  7.38 us

profile of v3, /device:TPU:0, one launch (start us, length us, event | category | flops | bytes accessed | tf_op | source)
XLA Modules:
  0.0 38.5 jit_solution(1862320316189532842)
XLA Ops:
  0.6 30.5 %expert.1 = (bf16[32,3072]{1,0:T(8,128)(2,1)S(1)}, bf16[32,3072]{1,0:T(8,128)(2,1)S(1)}, bf16[32,1024]{1,0:T(8,128)(2,1)S(1)}, bf16[32,1024]{1,0:T(8,128)(2,1)S(...) custom-call(bf16[1,3072]{1,0:T(2,128)(2,1)} %tokens_hbm.1, bf16[1,3072]{1,0:T(2,128)(2,1)} %cotan_hbm.1, ...), custom_call_target="tpu_custom_call" | custom-call | tf_op jit(solution)/shard_map/expert/pallas_call | solution.py:307
  31.2 7.4 %weights.1 = (bf16[3072,1024]{1,0:T(8,128)(2,1)}, bf16[3072,1024]{1,0:T(8,128)(2,1)}, bf16[1024,3072]{1,0:T(8,128)(2,1)}, bf16[1,3072]{1,0:T(2,128)(2,1)}, bf16[1,3072]{1,0:T(2,128)(2,1)}) custom-call(bf16[32,3072]{1,0:T(8,128)(2,1)S(1)} %get-tuple-element.16.tok, bf16[32,3072]{1,0:T(8,128)(2,1)S(1)} %get-tuple-element.17.cot, ...), custom_call_target="tpu_custom_call" | custom-call | tf_op jit(solution)/shard_map/weights/pallas_call | solution.py:352

commit v4 on v3

--- a/solution.py
+++ b/solution.py
@@ -207,7 +207,7 @@
                 device_id=peer(step), device_id_type=MESH,
             ).start()
 
-    unit = min(4, groups)
+    unit = min(2, groups)
     for p in range(n_pieces):
         for first in range(sum(sizes[:p]), sum(sizes[:p + 1]), unit):
             start = (first % groups) * LANES
@@ -252,7 +252,7 @@
 
 def weight_kernel(own, tok, cot, hid, ggp, gup, res, dg_hbm, du_hbm, dd_hbm, out, dtok, dg, du, dd, sem):
     model, hidden = dg.shape
-    tall = 192 if model % 192 == 0 else LANES
+    tall = 384 if model % 384 == 0 else LANES
     wide = min(LANES, hidden)
     n_tall, n_wide = model // tall, hidden // wide
     done = 0

time: 38.8 us -> 38.9 us (level)
  no operation moved by 1% of the time
where the time goes in v4:
time: 38.9 us; the launch traced here: 38.6 us
  Pallas kernels  38 us (98%)
  between operations  0.64 us (2%)
    pallas_call x1, Pallas kernels, on_device(): pl.pallas_call(functools.partial(expert_kernel, n_ep, n_tp, n_layers, own...  30.5 us
    pallas_call x1, Pallas kernels, on_device(): pl.pallas_call(functools.partial(weight_kernel, own), out_shape=(jax.Shap...  7.47 us

profile of v4, /device:TPU:0, one launch (start us, length us, event | category | flops | bytes accessed | tf_op | source)
XLA Modules:
  0.0 38.6 jit_solution(1852813891991427679)
XLA Ops:
  0.6 30.5 %expert.1 = (bf16[32,3072]{1,0:T(8,128)(2,1)S(1)}, bf16[32,3072]{1,0:T(8,128)(2,1)S(1)}, bf16[32,1024]{1,0:T(8,128)(2,1)S(1)}, bf16[32,1024]{1,0:T(8,128)(2,1)S(...) custom-call(bf16[1,3072]{1,0:T(2,128)(2,1)} %tokens_hbm.1, bf16[1,3072]{1,0:T(2,128)(2,1)} %cotan_hbm.1, ...), custom_call_target="tpu_custom_call" | custom-call | tf_op jit(solution)/shard_map/expert/pallas_call | solution.py:307
  31.2 7.5 %weights.1 = (bf16[3072,1024]{1,0:T(8,128)(2,1)}, bf16[3072,1024]{1,0:T(8,128)(2,1)}, bf16[1024,3072]{1,0:T(8,128)(2,1)}, bf16[1,3072]{1,0:T(2,128)(2,1)}, bf16[1,3072]{1,0:T(2,128)(2,1)}) custom-call(bf16[32,3072]{1,0:T(8,128)(2,1)S(1)} %get-tuple-element.16.tok, bf16[32,3072]{1,0:T(8,128)(2,1)S(1)} %get-tuple-element.17.cot, ...), custom_call_target="tpu_custom_call" | custom-call | tf_op jit(solution)/shard_map/weights/pallas_call | solution.py:352
